TPU v7x, 32 devices: a whole 2x2x4 slice. The times are simulated.
32 devices in a mesh: section: 4 (over z), dp: 8 (over y, x, core).
Axes of the slice: x: 2, y: 2, z: 4, core: 2. Of those that a mesh axis runs over, the one named last changes fastest.
Arguments:
- inputs: bfloat16 [2048, 2048], P('dp'), may hold values from -6 to 6
- order: int32 [8, 2], P('dp'), may hold values from 0 to 1, each once within a row
- image_start: int32 [8, 2], P('dp'), may hold values from 0 to 112, as said below
- image_len: int32 [8, 2], P('dp'), may hold values from 16 to 64
- norm_gain: float32 [4, 2048], P('section'), may hold values from 0.25 to 1.75
- qkv_weight: bfloat16 [4, 2048, 6144], P('section', 'dp'), may hold values from -0.125 to 0.125
- q_gain: float32 [4, 2048], P('section'), may hold values from 0.5 to 2.5
- k_gain: float32 [4, 2048], P('section'), may hold values from 0.5 to 2.5
- o_weight: bfloat16 [4, 2048, 2048], P('section'), may hold values from -0.125 to 0.125
Outputs:
- section_outputs: bfloat16 [4, 2048, 2048], P('section', 'dp')
Inputs may be any that keep to these rules, and one draw needn't show every extreme that they name: `order`: each row is a permutation of the micro-batch numbers. image_start + image_len <= 128 for every micro-batch.
All inputs are finite; a program needn't handle non-finite values.
Results may differ from a plain program's by a relative error of at most 0.035.
Values may be sent and summed in bfloat16 or wider, within the bound.
A program may use at most 128 MiB of HBM per device.

v0:
```python
import jax
import jax.numpy as jnp
from jax import lax
from jax.sharding import PartitionSpec as P

HEADS = 16
HEAD_DIM = 128


epsilon_value = 1e-05


def from_behind(shard, axis, by):
    devices = lax.axis_size(axis)
    pairs = [(i, i + by) for i in range(devices) if 0 <= i + by < devices]
    return lax.ppermute(shard, axis, pairs)


def normalize(hidden, gain):
    widened = hidden.astype(jnp.float32)
    mean_square = jnp.mean(widened * widened, axis=-1, keepdims=True)
    return (widened * lax.rsqrt(mean_square + epsilon_value) * gain).astype(jnp.bfloat16)


def head_norm(block, gain, seq_len):
    split = block.reshape(seq_len, HEADS, HEAD_DIM)
    mean_square = jnp.mean(split * split, axis=-1, keepdims=True)
    return (split * lax.rsqrt(mean_square + epsilon_value) * gain.reshape(HEADS, HEAD_DIM)).astype(
        jnp.bfloat16
    )


def finish(hidden, projected, gain_query, gain_key, out_weight, start, length):
    seq_len, model_width = hidden.shape
    queries = head_norm(projected[:, :model_width], gain_query, seq_len)
    key_rows = head_norm(projected[:, model_width : 2 * model_width], gain_key, seq_len)
    value_rows = (
        projected[:, 2 * model_width :].astype(jnp.bfloat16).reshape(seq_len, HEADS, HEAD_DIM)
    )
    scores = jnp.einsum(
        "qhd,khd->hqk", queries, key_rows, preferred_element_type=jnp.float32
    ) * HEAD_DIM ** (-0.5)
    position = jnp.arange(seq_len, dtype=jnp.int32)
    in_image = (position >= start) & (position < start + length)
    allowed = (position[None, :] <= position[:, None]) | in_image[:, None] & in_image[None, :]
    scores = jnp.where(allowed[None], scores, -1e30)
    row_max = jnp.max(scores, axis=-1, keepdims=True)
    lifted = jnp.exp(scores - row_max)
    probabilities = (lifted / jnp.sum(lifted, axis=-1, keepdims=True)).astype(jnp.bfloat16)
    mixed = jnp.einsum(
        "hqk,khd->qhd", probabilities, value_rows, preferred_element_type=jnp.float32
    )
    attended = mixed.reshape(seq_len, model_width).astype(jnp.bfloat16)
    output_rows = jnp.dot(attended, out_weight, preferred_element_type=jnp.float32)
    return (hidden.astype(jnp.float32) + output_rows).astype(jnp.bfloat16)


def body(inputs, order, image_start, image_len, norm_gain, qkv_weight, q_gain, k_gain, o_weight):
    section_count = lax.axis_size("section")
    section_index = lax.axis_index("section")
    micro_count = order.shape[1]
    row_count, model_width = inputs.shape
    seq_len = row_count // micro_count
    ordered = jnp.take(inputs.reshape(micro_count, seq_len, model_width), order[0], axis=0)
    starts = jnp.take(image_start[0], order[0])
    lengths = jnp.take(image_len[0], order[0])
    gain = norm_gain[0]
    gain_query = q_gain[0]
    gain_key = k_gain[0]
    out_weight = o_weight[0]
    shard = qkv_weight[0]
    turns = micro_count + section_count - 1

    def entering(turn_index, incoming):
        fresh = lax.dynamic_index_in_dim(
            ordered, jnp.clip(turn_index, 0, micro_count - 1), 0, keepdims=False
        )
        return jnp.where(section_index == 0, fresh, incoming)

    def settle(turn_index, hidden, project_rows, outputs):
        slot_index = turn_index - section_index
        active = (slot_index >= 0) & (slot_index < micro_count)
        chosen = jnp.clip(slot_index, 0, micro_count - 1)

        def compute(state):
            return finish(
                state,
                project_rows(state),
                gain_query,
                gain_key,
                out_weight,
                starts[chosen],
                lengths[chosen],
            )

        result = lax.cond(active, compute, lambda state: state, hidden)
        outputs = jnp.where(
            active, lax.dynamic_update_index_in_dim(outputs, result, chosen, 0), outputs
        )
        incoming = from_behind(result, "section", 1)
        return (incoming, outputs)

    outputs = jnp.zeros((micro_count, seq_len, model_width), jnp.bfloat16)
    incoming = jnp.zeros((seq_len, model_width), jnp.bfloat16)
    gathered = lax.all_gather(shard, "dp", axis=0, tiled=True)
    first_turn = 0

    def project(state):
        return jnp.dot(normalize(state, gain), gathered, preferred_element_type=jnp.float32)

    def advance(turn_index, carry):
        arriving, collected = carry
        hidden_now = entering(turn_index, arriving)
        return settle(turn_index, hidden_now, project, collected)

    incoming, outputs = lax.fori_loop(first_turn, turns, advance, (incoming, outputs))
    return outputs.reshape(1, row_count, model_width)


def solution(mesh):
    in_specs = (
        P("dp", None),
        P("dp", None),
        P("dp", None),
        P("dp", None),
        P("section", None),
        P("section", "dp", None),
        P("section", None),
        P("section", None),
        P("section", None, None),
    )
    out_specs = P("section", "dp", None)
    return jax.shard_map(body, mesh=mesh, in_specs=in_specs, out_specs=out_specs, check_vma=False)
```

profile of v0, /device:TPU:24, one launch (start us, length us, event | category | flops | bytes accessed | tf_op | source)
XLA Modules:
  0.0 386.1 jit_solution(17725801584185440760)
XLA Ops:
  13.6 121.8 %all-gather.3.cloned.1.call-done = bf16[1,2048,6144]{2,1,0:T(8,128)(2,1)} async-done(((bf16[1,256,6144]{2,1,0:T(8,128)(2,1)}), bf16[1,2048,6144]{2,1,0:T(8,128)(2,1)}) %all-gather.3.cloned.1.call-update) | async-done | bytes 25165840 | tf_op jit(solution)/shard_map/all_gather | solution.py:105
  136.6 242.7 %while.16 = (s32[]{:T(128)}, bf16[128,2048]{1,0:T(8,128)(2,1)S(1)}, bf16[2,128,2048]{2,1,0:T(8,128)(2,1)}, s32[]{:T(128)}, pred[]{:T(512)}, /*index=5*/bf16[2,12...) while((s32[]{:T(128)}, bf16[128,2048]{1,0:T(8,128)(2,1)S(1)}, ...), condition=%wide.region_8.10_spmd, body=%wide.region_0.9_spmd.sunk | while | flops 4437105152 | bytes 82521320 | solution.py:116
  139.0 2.0 fusion.27
  141.0 12.7 %collective-permute-done = bf16[128,2048]{1,0:T(8,128)(2,1)S(1)} collective-permute-done((bf16[128,2048]{1,0:T(8,128)(2,1)S(1)}, bf16[128,2048]{1,0:T(8,128)(2,1)S(1)}, u32[]{:S(2)}, u32[]{:S(2)}) %collective-permute-start) | collective-permute-done | bytes 524320 | tf_op jit(solution)/shard_map/while/body/eval_jaxpr/ppermute | solution.py:16
  156.1 2.0 fusion.27
  158.1 11.8 %collective-permute-done = bf16[128,2048]{1,0:T(8,128)(2,1)S(1)} collective-permute-done((bf16[128,2048]{1,0:T(8,128)(2,1)S(1)}, bf16[128,2048]{1,0:T(8,128)(2,1)S(1)}, u32[]{:S(2)}, u32[]{:S(2)}) %collective-permute-start) | collective-permute-done | bytes 524320 | tf_op jit(solution)/shard_map/while/body/eval_jaxpr/ppermute | solution.py:16
  172.4 2.0 fusion.27
  174.3 108.1 %collective-permute-done = bf16[128,2048]{1,0:T(8,128)(2,1)S(1)} collective-permute-done((bf16[128,2048]{1,0:T(8,128)(2,1)S(1)}, bf16[128,2048]{1,0:T(8,128)(2,1)S(1)}, u32[]{:S(2)}, u32[]{:S(2)}) %collective-permute-start) | collective-permute-done | bytes 524320 | tf_op jit(solution)/shard_map/while/body/eval_jaxpr/ppermute | solution.py:16
  283.5 33.5 %conditional.2 = (bf16[128,2048]{1,0:T(8,128)(2,1)S(1)}) conditional(s32[]{:T(128)} %convert_element_type.56, bf16[128,2048]{1,0:T(8,128)(2,1)S(1)} %bitcast_select_fusion.3, (bf16[128,2048]{1,0:T(8,128)(2,1)S(1)}, f32[1,2048]{1,0:T(1,128)S(1)}, bf16[2048,6144]{1,0:T(8,128)(2,1)}, s32[]{:T(128)}, s32[2]{0:T(128)S(1)}, /*index=5*/s32[2]{0:T(128)S(1)}, ...), branch_computations={%region_1.2_spmd, %region_2.8_spmd} | conditional | flops 4436580864 | bytes 77277576 | solution.py:96
  283.7 10.1 %fusion.8 = f32[128,6144]{1,0:T(8,128)S(1)} fusion(bf16[2048,6144]{1,0:T(8,128)(2,1)} %get-tuple-element.278, bf16[128,2048]{1,0:T(8,128)(2,1)S(1)} %get-tuple-element.276, f32[2048]{0:T(1024)S(1)} %bitcast.57, f32[128]{0:T(128)S(1)} %add_rsqrt_fusion.2), kind=kOutput, calls=%fused_computation.24 | convolution fusion | flops 3222274048 | bytes 28844544 | tf_op jit(solution)/shard_map/while/body/eval_jaxpr/cond/branch_1_fun/dot_general | solution.py:109
  293.9 1.7 copy-done.1
  296.7 2.8 slice_bitcast_fusion.1
  303.2 2.7 multiply_convert_fusion
  312.3 4.7 %fusion.1 = bf16[128,2048]{1,0:T(8,128)(2,1)S(1)} fusion(bf16[128,2048]{0,1:T(8,128)(2,1)S(1)} %bitcast.55, bf16[2048,2048]{1,0:T(8,128)(2,1)} %get-tuple-element.284, bf16[128,2048]{1,0:T(8,128)(2,1)S(1)} %get-tuple-element.276), kind=kOutput, calls=%fused_computation.5 | convolution fusion | flops 1074528256 | bytes 9961472 | tf_op jit(solution)/shard_map/while/body/eval_jaxpr/cond/branch_1_fun/dot_general | solution.py:54
  318.3 2.0 fusion.27
  320.3 11.0 %collective-permute-done = bf16[128,2048]{1,0:T(8,128)(2,1)S(1)} collective-permute-done((bf16[128,2048]{1,0:T(8,128)(2,1)S(1)}, bf16[128,2048]{1,0:T(8,128)(2,1)S(1)}, u32[]{:S(2)}, u32[]{:S(2)}) %collective-permute-start) | collective-permute-done | bytes 524320 | tf_op jit(solution)/shard_map/while/body/eval_jaxpr/ppermute | solution.py:16
  332.4 33.5 %conditional.2 = (bf16[128,2048]{1,0:T(8,128)(2,1)S(1)}) conditional(s32[]{:T(128)} %convert_element_type.56, bf16[128,2048]{1,0:T(8,128)(2,1)S(1)} %bitcast_select_fusion.3, (bf16[128,2048]{1,0:T(8,128)(2,1)S(1)}, f32[1,2048]{1,0:T(1,128)S(1)}, bf16[2048,6144]{1,0:T(8,128)(2,1)}, s32[]{:T(128)}, s32[2]{0:T(128)S(1)}, /*index=5*/s32[2]{0:T(128)S(1)}, ...), branch_computations={%region_1.2_spmd, %region_2.8_spmd} | conditional | flops 4436580864 | bytes 77277576 | solution.py:96
  332.6 10.1 %fusion.8 = f32[128,6144]{1,0:T(8,128)S(1)} fusion(bf16[2048,6144]{1,0:T(8,128)(2,1)} %get-tuple-element.278, bf16[128,2048]{1,0:T(8,128)(2,1)S(1)} %get-tuple-element.276, f32[2048]{0:T(1024)S(1)} %bitcast.57, f32[128]{0:T(128)S(1)} %add_rsqrt_fusion.2), kind=kOutput, calls=%fused_computation.24 | convolution fusion | flops 3222274048 | bytes 28844544 | tf_op jit(solution)/shard_map/while/body/eval_jaxpr/cond/branch_1_fun/dot_general | solution.py:109
  342.7 1.7 copy-done.1
  345.5 2.8 slice_bitcast_fusion.1
  352.0 2.7 multiply_convert_fusion
  361.2 4.7 %fusion.1 = bf16[128,2048]{1,0:T(8,128)(2,1)S(1)} fusion(bf16[128,2048]{0,1:T(8,128)(2,1)S(1)} %bitcast.55, bf16[2048,2048]{1,0:T(8,128)(2,1)} %get-tuple-element.284, bf16[128,2048]{1,0:T(8,128)(2,1)S(1)} %get-tuple-element.276), kind=kOutput, calls=%fused_computation.5 | convolution fusion | flops 1074528256 | bytes 9961472 | tf_op jit(solution)/shard_map/while/body/eval_jaxpr/cond/branch_1_fun/dot_general | solution.py:54
  367.2 2.0 fusion.27
  369.2 10.1 %collective-permute-done = bf16[128,2048]{1,0:T(8,128)(2,1)S(1)} collective-permute-done((bf16[128,2048]{1,0:T(8,128)(2,1)S(1)}, bf16[128,2048]{1,0:T(8,128)(2,1)S(1)}, u32[]{:S(2)}, u32[]{:S(2)}) %collective-permute-start) | collective-permute-done | bytes 524320 | tf_op jit(solution)/shard_map/while/body/eval_jaxpr/ppermute | solution.py:16
  (83 shorter events, 40.6 us)
Async XLA Ops:
  6.5 4.7 %copy-start = (bf16[256,2048]{1,0:T(8,128)(2,1)S(1)}, bf16[256,2048]{1,0:T(8,128)(2,1)}, u32[]{:S(2)}) copy-start(bf16[256,2048]{1,0:T(8,128)(2,1)} %param.15) | copy-start | bytes 3145732
  6.5 130.0 %copy-start.3 = (f32[1,2048]{1,0:T(1,128)S(1)}, f32[1,2048]{1,0:T(1,128)}, u32[]{:S(2)}) copy-start(f32[1,2048]{1,0:T(1,128)} %param.19) | copy-start | bytes 24580
  6.5 130.0 %copy-start.4 = (f32[1,2048]{1,0:T(1,128)S(1)}, f32[1,2048]{1,0:T(1,128)}, u32[]{:S(2)}) copy-start(f32[1,2048]{1,0:T(1,128)} %param.21) | copy-start | bytes 24580
  6.5 130.0 %copy-start.5 = (f32[1,2048]{1,0:T(1,128)S(1)}, f32[1,2048]{1,0:T(1,128)}, u32[]{:S(2)}) copy-start(f32[1,2048]{1,0:T(1,128)} %param.22) | copy-start | bytes 24580
  6.5 128.9 %all-gather.3.cloned.1.call-start = ((), (), s32[]{:S(2)}) async-start(), calls=%async_computation | async-start | bytes 28311552 | tf_op jit(solution)/shard_map/all_gather | solution.py:105
  137.7 16.0 %collective-permute-start = (bf16[128,2048]{1,0:T(8,128)(2,1)S(1)}, bf16[128,2048]{1,0:T(8,128)(2,1)S(1)}, u32[]{:S(2)}, u32[]{:S(2)}) collective-permute-start(bf16[128,2048]{1,0:T(8,128)(2,1)S(1)} %get-tuple-element.460), channel_id=1, source_target_pairs={{0,8},{8,16},{16,24},{1,9},{9,17},{17,25},{2,10},{10,18},{18,26},{... | collective-permute-start | bytes 1572872 | tf_op jit(solution)/shard_map/while/body/eval_jaxpr/ppermute | solution.py:16
  154.8 15.1 %collective-permute-start = (bf16[128,2048]{1,0:T(8,128)(2,1)S(1)}, bf16[128,2048]{1,0:T(8,128)(2,1)S(1)}, u32[]{:S(2)}, u32[]{:S(2)}) collective-permute-start(bf16[128,2048]{1,0:T(8,128)(2,1)S(1)} %get-tuple-element.460), channel_id=1, source_target_pairs={{0,8},{8,16},{16,24},{1,9},{9,17},{17,25},{2,10},{10,18},{18,26},{... | collective-permute-start | bytes 1572872 | tf_op jit(solution)/shard_map/while/body/eval_jaxpr/ppermute | solution.py:16
  171.1 111.4 %collective-permute-start = (bf16[128,2048]{1,0:T(8,128)(2,1)S(1)}, bf16[128,2048]{1,0:T(8,128)(2,1)S(1)}, u32[]{:S(2)}, u32[]{:S(2)}) collective-permute-start(bf16[128,2048]{1,0:T(8,128)(2,1)S(1)} %get-tuple-element.460), channel_id=1, source_target_pairs={{0,8},{8,16},{16,24},{1,9},{9,17},{17,25},{2,10},{10,18},{18,26},{... | collective-permute-start | bytes 1572872 | tf_op jit(solution)/shard_map/while/body/eval_jaxpr/ppermute | solution.py:16
  293.9 1.8 copy-start.1
  301.6 1.1 copy-start.2
  317.0 14.2 %collective-permute-start = (bf16[128,2048]{1,0:T(8,128)(2,1)S(1)}, bf16[128,2048]{1,0:T(8,128)(2,1)S(1)}, u32[]{:S(2)}, u32[]{:S(2)}) collective-permute-start(bf16[128,2048]{1,0:T(8,128)(2,1)S(1)} %get-tuple-element.460), channel_id=1, source_target_pairs={{0,8},{8,16},{16,24},{1,9},{9,17},{17,25},{2,10},{10,18},{18,26},{... | collective-permute-start | bytes 1572872 | tf_op jit(solution)/shard_map/while/body/eval_jaxpr/ppermute | solution.py:16
  342.7 1.8 copy-start.1
  350.4 1.1 copy-start.2
  365.9 13.4 %collective-permute-start = (bf16[128,2048]{1,0:T(8,128)(2,1)S(1)}, bf16[128,2048]{1,0:T(8,128)(2,1)S(1)}, u32[]{:S(2)}, u32[]{:S(2)}) collective-permute-start(bf16[128,2048]{1,0:T(8,128)(2,1)S(1)} %get-tuple-element.460), channel_id=1, source_target_pairs={{0,8},{8,16},{16,24},{1,9},{9,17},{17,25},{2,10},{10,18},{18,26},{... | collective-permute-start | bytes 1572872 | tf_op jit(solution)/shard_map/while/body/eval_jaxpr/ppermute | solution.py:16
Sparse Core Ops, SparseCore 0:
  9.2 126.1 all-gather.2
where the time goes:
time: 387 us; the launch traced here: 386 us
  waiting for transfers between devices  276 us (71%)
  matrix products  35.9 us (9%)
  other arithmetic  27.5 us (7%)
  local copies, waits for them, and re-layouts  23.8 us (6%)
  between operations  13.4 us (3%)
  starting transfers between devices  6.49 us (2%)
    ppermute x5, waiting for transfers between devices, from_behind(): return lax.ppermute(shard, axis, pairs)  154 us
    all_gather x1, waiting for transfers between devices, body(): gathered = lax.all_gather(shard, 'dp', axis=0, tiled=True)  122 us
    dot_general x2, matrix products, project(): jnp.dot(normalize(state, gain), gathered, preferred_element_type=jnp.floa...  20.2 us
    cond x14, local copies, waits for them, and re-layouts  14.4 us
    select_n x5, other arithmetic, settle(): jnp.where(active, lax.dynamic_update_index_in_dim(outputs, result, chosen...  9.84 us
    dot_general x2, matrix products, finish(): jnp.dot(attended, out_weight, preferred_element_type=jnp.float32)  9.39 us
  transfers between devices with their start and end apart: 6, of which 6 were waited for; matrix products, arithmetic and copies ran while one was open for 4% of the time, Pallas kernels for 0%

commit v1 on v0

v1 whole, which is shorter than its diff:
```python
import functools
import jax
import jax.numpy as jnp
from jax import lax
from jax.experimental import pallas as pl
from jax.experimental.pallas import tpu as pltpu
from jax.sharding import PartitionSpec as P

HEAD_DIM = 128
EPS = 1e-05
SUBS = 2
MESH = pl.DeviceIdType.MESH


def ring_order(chips):
    columns = 1
    while columns * columns < chips:
        columns *= 2
    rows = chips // columns
    cells = []
    for r in range(rows):
        line = list(range(1, columns))
        cells += [r * columns + c for c in (line if r % 2 == 0 else line[::-1])]
    cells += [r * columns for r in reversed(range(rows))]
    return cells


def look(table, index):
    found = jnp.int32(0)
    for i, value in enumerate(table):
        found = found + jnp.where(index == i, jnp.int32(value), jnp.int32(0))
    return found


def kernel(
    sections, devices, tile,
    order_ref, start_ref, len_ref, x_ref, gain_ref, w_ref, qg_ref, kg_ref, o_ref,
    out_ref,
    wbuf, obuf, xin, xout, acc, qkv, att,
    own_sem, o_sem, first_send, first_recv, ring_send, ring_recv, pair_send, pair_recv,
    hop_send, hop_recv,
):
    chips = devices // 2
    order = ring_order(chips)
    inverse = [order.index(c) for c in range(chips)]
    shard = w_ref.shape[0]
    piece = shard // (2 * SUBS)
    micro, chunks, seq, width = xin.shape
    model = chunks * width
    sec = lax.axis_index("section")
    me = lax.axis_index("dp")
    core = lax.rem(me, 2)
    place = look(inverse, me // 2)
    partner = me + 1 - 2 * core

    def at(offset):
        return look(order, lax.rem(place + (offset % chips), chips)) * 2 + core

    ahead, behind = at(1), at(-1)
    above = lax.rem(sec + 1, sections)
    below = lax.rem(sec + sections - 1, sections)

    barrier = pltpu.get_barrier_semaphore()
    for other in ((sec, ahead), (sec, behind), (sec, partner), (above, me), (below, me)):
        pl.semaphore_signal(barrier, inc=1, device_id=other, device_id_type=MESH)
    pl.semaphore_wait(barrier, 5)

    own_rows = pl.ds(pl.multiple_of(me * shard, shard), shard)

    def rows(owner, way, sub):
        return pl.ds(pl.multiple_of(owner * shard + (way * SUBS + sub) * piece, piece), piece)

    def ring_copy(way, sub, step):
        owner = at(-step if way == 0 else step)
        where = rows(owner, way, sub)
        if step == 0:
            source = w_ref.at[pl.ds((way * SUBS + sub) * piece, piece)]
        else:
            source = wbuf.at[where]
        return pltpu.make_async_remote_copy(
            src_ref=source, dst_ref=wbuf.at[where],
            send_sem=ring_send.at[way, sub, step], recv_sem=ring_recv.at[way, sub, step],
            device_id=(sec, ahead if way == 0 else behind), device_id_type=MESH,
        )

    def pair_copy(way, sub, step):
        owner = at(-step if way == 0 else step)
        where = rows(owner, way, sub)
        return pltpu.make_async_remote_copy(
            src_ref=wbuf.at[where], dst_ref=wbuf.at[where],
            send_sem=pair_send.at[way, sub, step - 1], recv_sem=pair_recv.at[way, sub, step - 1],
            device_id=(sec, partner), device_id_type=MESH,
        )

    ring = {}
    pair = {}
    for sub in range(SUBS):
        for way in range(2):
            ring[way, sub, 0] = ring_copy(way, sub, 0)
            ring[way, sub, 0].start()
    first = pltpu.make_async_remote_copy(
        src_ref=w_ref, dst_ref=wbuf.at[own_rows], send_sem=first_send, recv_sem=first_recv,
        device_id=(sec, partner), device_id_type=MESH,
    )
    first.start()
    own = pltpu.make_async_copy(w_ref, wbuf.at[own_rows], own_sem)
    own.start()
    o_copy = pltpu.make_async_copy(o_ref, obuf, o_sem)
    o_copy.start()
    for step in range(1, chips):
        for sub in range(SUBS):
            for way in range(2):
                ring[way, sub, step - 1].wait_recv()
                if step < chips - 1:
                    ring[way, sub, step] = ring_copy(way, sub, step)
                    ring[way, sub, step].start()
                pair[way, sub, step] = pair_copy(way, sub, step)
                pair[way, sub, step].start()
    own.wait()
    o_copy.wait()
    first.wait()
    for step in range(1, chips):
        for sub in range(SUBS):
            for way in range(2):
                pair[way, sub, step].wait()
                ring[way, sub, step - 1].wait_send()

    def hop(j, c):
        return pltpu.make_async_remote_copy(
            src_ref=xout.at[j, c], dst_ref=xin.at[j, c],
            send_sem=hop_send.at[j, c], recv_sem=hop_recv.at[j, c],
            device_id=(above, me), device_id_type=MESH,
        )

    total = w_ref.shape[1]
    row_id = lax.broadcasted_iota(jnp.int32, (seq, seq), 0)
    col_id = lax.broadcasted_iota(jnp.int32, (seq, seq), 1)
    per_tile = tile // HEAD_DIM

    @pl.loop(0, micro)
    def _(j):
        which = order_ref[0, j]
        s0 = start_ref[0, which]
        s1 = s0 + len_ref[0, which]

        square = jnp.zeros((seq, 1), jnp.float32)
        for c in range(chunks):
            span = slice(c * width, (c + 1) * width)

            @pl.when(sec == 0)
            def _():
                xin[j, c] = x_ref[which, :, span]

            @pl.when(sec > 0)
            def _():
                hop(j, c).wait_recv()

            wide = xin[j, c].astype(jnp.float32)
            square = square + jnp.sum(wide * wide, axis=-1, keepdims=True)
            scaled = (wide * gain_ref[:, span]).astype(jnp.bfloat16)

            @pl.loop(0, total // tile)
            def _(n):
                cols = pl.ds(pl.multiple_of(n * tile, tile), tile)
                part = jnp.dot(scaled, wbuf[span, cols], preferred_element_type=jnp.float32)
                if c == 0:
                    acc[:, cols] = part
                else:
                    acc[:, cols] += part

        scale = lax.rsqrt(square * (1.0 / model) + EPS)

        for part, gains in ((0, qg_ref), (1, kg_ref)):
            @pl.loop(0, model // tile)
            def _(n):
                for i in range(per_tile):
                    here = pl.ds(pl.multiple_of(n * tile + i * HEAD_DIM, HEAD_DIM), HEAD_DIM)
                    cols = pl.ds(
                        pl.multiple_of(part * model + n * tile + i * HEAD_DIM, HEAD_DIM), HEAD_DIM
                    )
                    p = acc[:, cols] * scale
                    mean = jnp.mean(p * p, axis=-1, keepdims=True)
                    qkv[:, cols] = (p * lax.rsqrt(mean + EPS) * gains[:, here]).astype(jnp.bfloat16)

        allowed = (col_id <= row_id) | (
            (row_id >= s0) & (row_id < s1) & (col_id >= s0) & (col_id < s1)
        )

        @pl.loop(0, model // tile)
        def _(n):
            for i in range(per_tile):
                base = n * tile + i * HEAD_DIM
                here = pl.ds(pl.multiple_of(base, HEAD_DIM), HEAD_DIM)
                q = qkv[:, here]
                k = qkv[:, pl.ds(pl.multiple_of(model + base, HEAD_DIM), HEAD_DIM)]
                v = acc[:, pl.ds(pl.multiple_of(2 * model + base, HEAD_DIM), HEAD_DIM)] * scale
                scores = lax.dot_general(
                    q, k, (((1,), (1,)), ((), ())), preferred_element_type=jnp.float32
                ) * HEAD_DIM ** (-0.5)
                scores = jnp.where(allowed, scores, -1e30)
                lifted = jnp.exp(scores - jnp.max(scores, axis=-1, keepdims=True))
                weights = lifted / jnp.sum(lifted, axis=-1, keepdims=True)
                att[:, here] = jnp.dot(
                    weights.astype(jnp.bfloat16), v.astype(jnp.bfloat16),
                    preferred_element_type=jnp.float32,
                ).astype(jnp.bfloat16)

        for c in range(chunks):
            span = slice(c * width, (c + 1) * width)
            grown = jnp.dot(att[...], obuf[:, span], preferred_element_type=jnp.float32)
            fresh = (xin[j, c].astype(jnp.float32) + grown).astype(jnp.bfloat16)
            xout[j, c] = fresh
            out_ref[j, :, span] = fresh

            @pl.when(sec < sections - 1)
            def _():
                hop(j, c).start()

    @pl.when(sec < sections - 1)
    def _():
        for j in range(micro):
            for c in range(chunks):
                hop(j, c).wait_send()


def solution(mesh):
    sections, devices = mesh.shape["section"], mesh.shape["dp"]

    def body(inputs, order, image_start, image_len, norm_gain, qkv_weight, q_gain, k_gain, o_weight):
        micro = order.shape[1]
        count, model = inputs.shape
        seq = count // micro
        total = qkv_weight.shape[2]
        shard = qkv_weight.shape[1]
        width = tile = model // 4
        chunks = model // width
        chips = devices // 2
        smem = pl.BlockSpec(memory_space=pltpu.SMEM)
        vmem = pl.BlockSpec(memory_space=pltpu.VMEM)
        hbm = pl.BlockSpec(memory_space=pltpu.HBM)
        dma = pltpu.SemaphoreType.DMA
        out = pl.pallas_call(
            functools.partial(kernel, sections, devices, tile),
            out_shape=jax.ShapeDtypeStruct((micro, seq, model), jnp.bfloat16),
            in_specs=[smem, smem, smem, vmem, vmem, hbm, vmem, vmem, hbm],
            out_specs=vmem,
            scratch_shapes=[
                pltpu.VMEM((model, total), jnp.bfloat16),
                pltpu.VMEM((model, model), jnp.bfloat16),
                pltpu.VMEM((micro, chunks, seq, width), jnp.bfloat16),
                pltpu.VMEM((micro, chunks, seq, width), jnp.bfloat16),
                pltpu.VMEM((seq, total), jnp.float32),
                pltpu.VMEM((seq, 2 * model), jnp.bfloat16),
                pltpu.VMEM((seq, model), jnp.bfloat16),
                dma, dma, dma, dma,
                dma((2, SUBS, chips - 1)),
                dma((2, SUBS, chips - 1)),
                dma((2, SUBS, chips - 1)),
                dma((2, SUBS, chips - 1)),
                dma((micro, chunks)),
                dma((micro, chunks)),
            ],
            compiler_params=pltpu.CompilerParams(
                collective_id=0, has_side_effects=True, vmem_limit_bytes=60 * 1024 * 1024
            ),
        )(
            order, image_start, image_len, inputs.reshape(micro, seq, model), norm_gain,
            qkv_weight.reshape(shard, total), q_gain, k_gain, o_weight.reshape(model, model),
        )
        return out.reshape(1, count, model)

    in_specs = (
        P("dp", None),
        P("dp", None),
        P("dp", None),
        P("dp", None),
        P("section", None),
        P("section", "dp", None),
        P("section", None),
        P("section", None),
        P("section", None, None),
    )
    out_specs = P("section", "dp", None)
    return jax.shard_map(body, mesh=mesh, in_specs=in_specs, out_specs=out_specs, check_vma=False)
```

time: 387 us -> 229 us (0.59)
  waiting for transfers between devices: 276 us -> 0 us
  Pallas kernels: 0 us -> 226 us
  matrix products: 35.9 us -> 0 us
  other arithmetic: 27.5 us -> 0 us
  local copies, waits for them, and re-layouts: 23.8 us -> 2.3 us
  between operations: 13.4 us -> 0.01 us
  starting transfers between devices: 6.49 us -> 0 us
    pallas_call x0 -> x1, Pallas kernels: none -> 226 us  [body(): pl.pallas_call(functools.partial(kernel, sections, devices, tile), out_sh...]
    ppermute x5 -> x0, waiting for transfers between devices: 154 us -> none  [from_behind(): return lax.ppermute(shard, axis, pairs)]
    all_gather x1 -> x0, waiting for transfers between devices: 122 us -> none  [body(): gathered = lax.all_gather(shard, 'dp', axis=0, tiled=True)]
    dot_general x8 -> x0, matrix products: 35.9 us -> none  [the longest x2 20.2 us: project(): jnp.dot(normalize(state, gain), gathered, preferred_element_type=jnp.floa...]
    select_n x15 -> x0, other arithmetic: 18.5 us -> none  [the longest x5 9.84 us: settle(): jnp.where(active, lax.dynamic_update_index_in_dim(outputs, result, chosen...]
    cond x14 -> x0, local copies, waits for them, and re-layouts: 14.4 us -> none
    ppermute x5 -> x0, starting transfers between devices: 6.46 us -> none  [from_behind(): return lax.ppermute(shard, axis, pairs)]
    convert_element_type x2 -> x0, other arithmetic: 5.38 us -> none  [head_norm(): (split * lax.rsqrt(mean_square + epsilon_value) * gain.reshape(HEADS, HEA...]
  transfers between devices with their start and end apart: 6 -> 0, of which waited for: 6 -> 0; matrix products, arithmetic and copies ran while one was open for 4% -> 0% of each run, Pallas kernels for 0% -> 0%
where the time goes in v1:
time: 229 us; the launch traced here: 228 us
  Pallas kernels  226 us (99%)
  local copies, waits for them, and re-layouts  2.3 us (1%)
    pallas_call x1, Pallas kernels, body(): pl.pallas_call(functools.partial(kernel, sections, devices, tile), out_sh...  226 us

profile of v1, /device:TPU:24, one launch (start us, length us, event | category | flops | bytes accessed | tf_op | source)
XLA Modules:
  0.0 228.5 jit_solution(1551180780544962982)
XLA Ops:
  0.0 226.2 %shard_map.91 = bf16[2,128,2048]{2,1,0:T(8,128)(2,1)} custom-call(s32[1,2]{1,0:T(1,128)} %order_ref.1, s32[1,2]{1,0:T(1,128)} %start_ref.1, s32[1,2]{1,0:T(1,128)} %len_ref.1, bf16[2,128,2048]{2,1,0:T(8,128)(2,1)} %bitcast.7, f32[1,2048]{1,0:T(1,128)} %gain_ref.1, bf16[256,6144]{1,0:T(8,128)(2,1)} %bitcast.6, f32[1,2048]{1,0:T(1,128)} %qg_ref.1, ...), custom_call_target="tpu_custom_call" | custom-call | tf_op jit(solution)/shard_map/pallas_call | solution.py:242
  226.2 2.3 %copy.11 = bf16[1,256,2048]{2,1,0:T(8,128)(2,1)} copy(bf16[1,256,2048]{2,1,0:T(8,128)(2,1)} %bitcast.5) | data formatting | bytes 2097152

commit v2 on v1

--- a/solution.py
+++ b/solution.py
@@ -8,7 +8,13 @@
 
 HEAD_DIM = 128
 EPS = 1e-05
+LOG2_E = 1.4426950408889634
 SUBS = 2
+CHUNKS = 4
+WIDE = 1
+EARLY_WIDE = 3
+HEADS_AT_ONCE = 16
+NORMS_AT_ONCE = 16
 MESH = pl.DeviceIdType.MESH
 
 
@@ -33,10 +39,10 @@
 
 
 def kernel(
-    sections, devices, tile,
+    sections, devices,
     order_ref, start_ref, len_ref, x_ref, gain_ref, w_ref, qg_ref, kg_ref, o_ref,
     out_ref,
-    wbuf, obuf, xin, xout, acc, qkv, att,
+    wbuf, obuf, xin, xout, acc, qkv, att, early,
     own_sem, o_sem, first_send, first_recv, ring_send, ring_recv, pair_send, pair_recv,
     hop_send, hop_recv,
 ):
@@ -107,6 +113,43 @@
     own.start()
     o_copy = pltpu.make_async_copy(o_ref, obuf, o_sem)
     o_copy.start()
+    total = w_ref.shape[1]
+    half = shard // 2
+
+    @pl.when(sec == 0)
+    def _():
+        for j in range(micro):
+            for n in range(model // half):
+                part = x_ref[order_ref[0, j], :, n * half : (n + 1) * half].astype(jnp.float32)
+                early[n, j * seq : (j + 1) * seq] = (
+                    part * gain_ref[:, n * half : (n + 1) * half]
+                ).astype(jnp.bfloat16)
+
+    def absorb(halves, fresh=False):
+        @pl.when(sec == 0)
+        def _():
+            @pl.loop(0, EARLY_WIDE)
+            def _(n):
+                cols = pl.ds(pl.multiple_of(n * (total // EARLY_WIDE), total // EARLY_WIDE), total // EARLY_WIDE)
+                left = [early[h] for h in halves]
+                right = [wbuf[pl.ds(pl.multiple_of(h * half, half), half), cols] for h in halves]
+                if half % 128 == 0:
+                    left = [jnp.concatenate(left, axis=1)]
+                    right = [jnp.concatenate(right, axis=0)]
+                for i, (one, other) in enumerate(zip(left, right)):
+                    part = jnp.dot(one, other, preferred_element_type=jnp.float32)
+                    if fresh and i == 0:
+                        acc[:, cols] = part
+                    else:
+                        acc[:, cols] += part
+
+    def mate(owner):
+        return owner + 1 - 2 * core
+
+    own.wait()
+    first.wait_recv()
+    absorb([2 * me, 2 * me + 1], fresh=True)
+    absorb([2 * partner, 2 * partner + 1])
     for step in range(1, chips):
         for sub in range(SUBS):
             for way in range(2):
@@ -116,13 +159,17 @@
                     ring[way, sub, step].start()
                 pair[way, sub, step] = pair_copy(way, sub, step)
                 pair[way, sub, step].start()
-    own.wait()
+        for way in range(2):
+            for sub in range(SUBS):
+                pair[way, sub, step].wait_recv()
+            owner = at(-step if way == 0 else step)
+            absorb([2 * owner + way, 2 * mate(owner) + way])
     o_copy.wait()
-    first.wait()
+    first.wait_send()
     for step in range(1, chips):
         for sub in range(SUBS):
             for way in range(2):
-                pair[way, sub, step].wait()
+                pair[way, sub, step].wait_send()
                 ring[way, sub, step - 1].wait_send()
 
     def hop(j, c):
@@ -132,10 +179,8 @@
             device_id=(above, me), device_id_type=MESH,
         )
 
-    total = w_ref.shape[1]
     row_id = lax.broadcasted_iota(jnp.int32, (seq, seq), 0)
     col_id = lax.broadcasted_iota(jnp.int32, (seq, seq), 1)
-    per_tile = tile // HEAD_DIM
 
     @pl.loop(0, micro)
     def _(j):
@@ -143,6 +188,7 @@
         s0 = start_ref[0, which]
         s1 = s0 + len_ref[0, which]
 
+        own_seq = pl.ds(pl.multiple_of(j * seq, seq), seq)
         square = jnp.zeros((seq, 1), jnp.float32)
         for c in range(chunks):
             span = slice(c * width, (c + 1) * width)
@@ -159,51 +205,55 @@
             square = square + jnp.sum(wide * wide, axis=-1, keepdims=True)
             scaled = (wide * gain_ref[:, span]).astype(jnp.bfloat16)
 
-            @pl.loop(0, total // tile)
+            @pl.when(sec > 0)
+            def _():
+                @pl.loop(0, WIDE)
+                def _(n):
+                    cols = pl.ds(pl.multiple_of(n * (total // WIDE), total // WIDE), total // WIDE)
+                    part = jnp.dot(scaled, wbuf[span, cols], preferred_element_type=jnp.float32)
+                    if c == 0:
+                        acc[own_seq, cols] = part
+                    else:
+                        acc[own_seq, cols] += part
+
+        scale = lax.rsqrt(square * (1.0 / model) + EPS)
+
+        for part, gains in ((0, qg_ref), (1, kg_ref)):
+            factor = HEAD_DIM ** (-0.5) * LOG2_E if part == 0 else 1.0
+
+            @pl.loop(0, model // (NORMS_AT_ONCE * HEAD_DIM))
             def _(n):
-                cols = pl.ds(pl.multiple_of(n * tile, tile), tile)
-                part = jnp.dot(scaled, wbuf[span, cols], preferred_element_type=jnp.float32)
-                if c == 0:
-                    acc[:, cols] = part
-                else:
-                    acc[:, cols] += part
-
-        scale = lax.rsqrt(square * (1.0 / model) + EPS)
-
-        for part, gains in ((0, qg_ref), (1, kg_ref)):
-            @pl.loop(0, model // tile)
-            def _(n):
-                for i in range(per_tile):
-                    here = pl.ds(pl.multiple_of(n * tile + i * HEAD_DIM, HEAD_DIM), HEAD_DIM)
-                    cols = pl.ds(
-                        pl.multiple_of(part * model + n * tile + i * HEAD_DIM, HEAD_DIM), HEAD_DIM
-                    )
-                    p = acc[:, cols] * scale
-                    mean = jnp.mean(p * p, axis=-1, keepdims=True)
-                    qkv[:, cols] = (p * lax.rsqrt(mean + EPS) * gains[:, here]).astype(jnp.bfloat16)
+                for i in range(NORMS_AT_ONCE):
+                    base = (n * NORMS_AT_ONCE + i) * HEAD_DIM
+                    here = pl.ds(pl.multiple_of(base, HEAD_DIM), HEAD_DIM)
+                    cols = pl.ds(pl.multiple_of(part * model + base, HEAD_DIM), HEAD_DIM)
+                    p = acc[own_seq, cols]
+                    mean = jnp.mean(p * p, axis=-1, keepdims=True) * scale * scale
+                    lift = lax.rsqrt(mean + EPS) * scale
+                    qkv[:, cols] = (p * lift * (gains[:, here] * factor)).astype(jnp.bfloat16)
 
         allowed = (col_id <= row_id) | (
             (row_id >= s0) & (row_id < s1) & (col_id >= s0) & (col_id < s1)
         )
 
-        @pl.loop(0, model // tile)
+        @pl.loop(0, model // (HEADS_AT_ONCE * HEAD_DIM))
         def _(n):
-            for i in range(per_tile):
-                base = n * tile + i * HEAD_DIM
+            for i in range(HEADS_AT_ONCE):
+                base = (n * HEADS_AT_ONCE + i) * HEAD_DIM
                 here = pl.ds(pl.multiple_of(base, HEAD_DIM), HEAD_DIM)
                 q = qkv[:, here]
                 k = qkv[:, pl.ds(pl.multiple_of(model + base, HEAD_DIM), HEAD_DIM)]
-                v = acc[:, pl.ds(pl.multiple_of(2 * model + base, HEAD_DIM), HEAD_DIM)] * scale
+                v = acc[own_seq, pl.ds(pl.multiple_of(2 * model + base, HEAD_DIM), HEAD_DIM)] * scale
                 scores = lax.dot_general(
                     q, k, (((1,), (1,)), ((), ())), preferred_element_type=jnp.float32
-                ) * HEAD_DIM ** (-0.5)
-                scores = jnp.where(allowed, scores, -1e30)
-                lifted = jnp.exp(scores - jnp.max(scores, axis=-1, keepdims=True))
-                weights = lifted / jnp.sum(lifted, axis=-1, keepdims=True)
-                att[:, here] = jnp.dot(
-                    weights.astype(jnp.bfloat16), v.astype(jnp.bfloat16),
+                )
+                lifted = jnp.where(allowed, jnp.exp2(scores), 0.0)
+                mixed = jnp.dot(
+                    lifted.astype(jnp.bfloat16), v.astype(jnp.bfloat16),
                     preferred_element_type=jnp.float32,
-                ).astype(jnp.bfloat16)
+                )
+                share = 1.0 / jnp.sum(lifted, axis=-1, keepdims=True)
+                att[:, here] = (mixed * share).astype(jnp.bfloat16)
 
         for c in range(chunks):
             span = slice(c * width, (c + 1) * width)
@@ -232,7 +282,7 @@
         seq = count // micro
         total = qkv_weight.shape[2]
         shard = qkv_weight.shape[1]
-        width = tile = model // 4
+        width = model // CHUNKS
         chunks = model // width
         chips = devices // 2
         smem = pl.BlockSpec(memory_space=pltpu.SMEM)
@@ -240,7 +290,7 @@
         hbm = pl.BlockSpec(memory_space=pltpu.HBM)
         dma = pltpu.SemaphoreType.DMA
         out = pl.pallas_call(
-            functools.partial(kernel, sections, devices, tile),
+            functools.partial(kernel, sections, devices),
             out_shape=jax.ShapeDtypeStruct((micro, seq, model), jnp.bfloat16),
             in_specs=[smem, smem, smem, vmem, vmem, hbm, vmem, vmem, hbm],
             out_specs=vmem,
@@ -249,9 +299,10 @@
                 pltpu.VMEM((model, model), jnp.bfloat16),
                 pltpu.VMEM((micro, chunks, seq, width), jnp.bfloat16),
                 pltpu.VMEM((micro, chunks, seq, width), jnp.bfloat16),
-                pltpu.VMEM((seq, total), jnp.float32),
+                pltpu.VMEM((count, total), jnp.float32),
                 pltpu.VMEM((seq, 2 * model), jnp.bfloat16),
                 pltpu.VMEM((seq, model), jnp.bfloat16),
+                pltpu.VMEM((2 * model // shard, count, shard // 2), jnp.bfloat16),
                 dma, dma, dma, dma,
                 dma((2, SUBS, chips - 1)),
                 dma((2, SUBS, chips - 1)),

time: 229 us -> 183 us (0.80)
  Pallas kernels: 226 us -> 181 us
    pallas_call x1, Pallas kernels: 226 us -> 181 us  [body(): pl.pallas_call(functools.partial(kernel, sections, devices), out_shape=ja...]
where the time goes in v2:
time: 183 us
  Pallas kernels  181 us (99%)
  local copies, waits for them, and re-layouts  2.3 us (1%)
    pallas_call x1, Pallas kernels, body(): pl.pallas_call(functools.partial(kernel, sections, devices), out_shape=ja...  181 us

profile of v2, /device:TPU:24, one launch (start us, length us, event | category | flops | bytes accessed | tf_op | source)
XLA Modules:
  0.0 183.1 jit_solution(8575920020630544142)
XLA Ops:
  0.0 180.8 %shard_map.91 = bf16[2,128,2048]{2,1,0:T(8,128)(2,1)} custom-call(s32[1,2]{1,0:T(1,128)} %order_ref.1, s32[1,2]{1,0:T(1,128)} %start_ref.1, s32[1,2]{1,0:T(1,128)} %len_ref.1, bf16[2,128,2048]{2,1,0:T(8,128)(2,1)} %bitcast.7, f32[1,2048]{1,0:T(1,128)} %gain_ref.1, bf16[256,6144]{1,0:T(8,128)(2,1)} %bitcast.6, f32[1,2048]{1,0:T(1,128)} %qg_ref.1, ...), custom_call_target="tpu_custom_call" | custom-call | tf_op jit(solution)/shard_map/pallas_call | solution.py:292
  180.8 2.3 %copy.11 = bf16[1,256,2048]{2,1,0:T(8,128)(2,1)} copy(bf16[1,256,2048]{2,1,0:T(8,128)(2,1)} %bitcast.5) | data formatting | bytes 2097152
